TPU v7x, 32 devices: a whole 2x2x4 slice. The times are simulated.
32 devices in a mesh: fsdp: 8 (over z, y), tp: 4 (over x, core).
Axes of the slice: x: 2, y: 2, z: 4, core: 2. Of those that a mesh axis runs over, the one named last changes fastest.
Arguments:
- base_o: bfloat16 [2, 8192, 8192], P(None, 'tp', 'fsdp'), may hold values from -0.0625 to 0.0625
- base_down: bfloat16 [2, 28672, 8192], P(None, 'tp', 'fsdp'), may hold values from -0.03125 to 0.03125
- factor_a_o: bfloat16 [2, 64, 4, 2048], P(None, None, None, 'fsdp'), may hold values from -0.0625 to 0.0625
- factor_b_o: bfloat16 [2, 8192, 64], P(None, 'fsdp'), may hold values from -1.1953125 to 1.1953125
- factor_a_down: bfloat16 [2, 64, 4, 7168], P(None, None, None, 'fsdp'), may hold values from -0.03125 to 0.03125
- factor_b_down: bfloat16 [2, 8192, 64], P(None, 'fsdp'), may hold values from -1.1953125 to 1.1953125
- magnitude_o: float32 [2, 8192], P(None, 'fsdp'), may hold values from 30 to 300
- magnitude_down: float32 [2, 8192], P(None, 'fsdp'), may hold values from 30 to 300
Outputs:
- merged_o: bfloat16 [2, 8192, 8192], P(None, 'tp', 'fsdp')
- merged_down: bfloat16 [2, 28672, 8192], P(None, 'tp', 'fsdp')
All inputs are finite; a program needn't handle non-finite values.
Results may differ from a plain program's by a relative error of at most 0.001.
Values may be sent and summed in bfloat16 or wider, within the bound.
A program may use at most 192 MiB of HBM per device.

v0:
```python
import jax
import jax.numpy as jnp
from jax import lax
from jax.sharding import PartitionSpec as P


def low_rank(rows_a, factor_b):
    return jnp.einsum("lri,lor->lio", rows_a, factor_b, preferred_element_type=jnp.float32)


def squares(base, delta):
    summed = base.astype(jnp.float32) + 0.25 * delta
    return (summed, jnp.sum(summed * summed, axis=1))


def finish(summed, square, magnitude):
    return (magnitude[:, None, :] * summed * lax.rsqrt(square + 1e-06)[:, None, :]).astype(
        jnp.bfloat16
    )


def local(
    base_o,
    base_down,
    factor_a_o,
    factor_b_o,
    factor_a_down,
    factor_b_down,
    magnitude_o,
    magnitude_down,
):
    column_t = lax.axis_index("tp")
    own_o = lax.dynamic_index_in_dim(factor_a_o, column_t, 2, keepdims=False)
    delta_o = low_rank(lax.all_gather(own_o, "fsdp", axis=2, tiled=True), factor_b_o)
    own_down = lax.dynamic_index_in_dim(factor_a_down, column_t, 2, keepdims=False)
    delta_down = low_rank(lax.all_gather(own_down, "fsdp", axis=2, tiled=True), factor_b_down)
    summed_o, partial_o = squares(base_o, delta_o)
    square_o = lax.psum(partial_o, "tp")
    merged_o = finish(summed_o, square_o, magnitude_o)
    summed_down, partial_down = squares(base_down, delta_down)
    square_down = lax.psum(partial_down, "tp")
    merged_down = finish(summed_down, square_down, magnitude_down)
    return (merged_o, merged_down)


def solution(mesh):
    return jax.shard_map(
        local,
        mesh=mesh,
        in_specs=(
            P(None, "tp", "fsdp"),
            P(None, "tp", "fsdp"),
            P(None, None, None, "fsdp"),
            P(None, "fsdp", None),
            P(None, None, None, "fsdp"),
            P(None, "fsdp", None),
            P(None, "fsdp"),
            P(None, "fsdp"),
        ),
        out_specs=(P(None, "tp", "fsdp"), P(None, "tp", "fsdp")),
        check_vma=False,
    )
```

profile of v0, /device:TPU:0, one launch (start us, length us, event | category | flops | bytes accessed | tf_op | source)
XLA Modules:
  0.0 159.7 jit_solution(17813612528903440651)
XLA Ops:
  7.2 0.0 copy-start
  7.2 0.0 copy-start.2
  7.2 0.0 all-gather.4.cloned.1.call-start
  7.2 1.1 copy-done
  8.4 0.5 constant_dynamic-slice_fusion
  8.8 0.7 copy.13
  9.5 0.0 all-gather.4.cloned.1.call-update
  9.6 1.1 constant_dynamic-slice_fusion.1
  10.7 33.7 %all-gather = bf16[2,64,1,2048]{3,1,0,2:T(8,128)(2,1)S(1)} all-gather(bf16[2,64,1,256]{3,1,0,2:T(8,128)(2,1)S(1)} %copy.12), channel_id=2, replica_groups=mesh['fsdp'=8,'tp'=4] {'fsdp'}, dimensions={3}, use_global_device_ids=true | all-gather | bytes 589824 | tf_op jit(solution)/shard_map/all_gather | solution.py:34
  44.4 10.1 %multiply_reduce_fusion.1 = (f32[2,1024]{1,0:T(2,128)S(1)}, f32[2,2048,1024]{2,1,0:T(8,128)}) fusion(bf16[2,2048,1024]{2,1,0:T(8,128)(2,1)} %param.8, bf16[2,1024,64]{1,2,0:T(8,128)(2,1)} %param.11, bf16[2,64,1,2048]{3,1,0,2:T(8,128)(2,1)S(1)} %all-gather), kind=kOutput, calls=%fused_computation.4 | convolution fusion | flops 557840384 | bytes 25960448 | tf_op jit(solution)/shard_map/lri,lor->lio/dot_general | solution.py:8
  54.5 0.0 copy-start.4
  54.5 7.0 %all-gather.4.cloned.1.call-done = bf16[2,64,1,7168]{3,1,0,2:T(8,128)(2,1)} async-done(((bf16[2,64,1,896]{3,1,0,2:T(8,128)(2,1)}), bf16[2,64,1,7168]{3,1,0,2:T(8,128)(2,1)}) %all-gather.4.cloned.1.call-update) | async-done | bytes 1835024 | tf_op jit(solution)/shard_map/all_gather | solution.py:36
  61.5 0.0 copy-done.2
  61.5 30.8 %multiply_reduce_fusion = (f32[2,1024]{1,0:T(2,128)S(1)}, f32[2,7168,1024]{2,1,0:T(8,128)}) fusion(bf16[2,7168,1024]{2,1,0:T(8,128)(2,1)} %param.9, bf16[2,1024,64]{1,2,0:T(8,128)(2,1)S(1)} %copy-done.2, bf16[2,64,1,7168]{3,1,0,2:T(8,128)(2,1)} %all-gather.4.cloned.1.call-done), kind=kOutput, calls=%fused_computation.1 | convolution fusion | flops 1952446464 | bytes 90185728 | tf_op jit(solution)/shard_map/lri,lor->lio/dot_general | solution.py:8
  92.3 10.1 %all-reduce = (f32[2,1024]{1,0:T(2,128)S(1)}, f32[2,1024]{1,0:T(2,128)S(1)}) all-reduce(f32[2,1024]{1,0:T(2,128)S(1)} %get-tuple-element.4, f32[2,1024]{1,0:T(2,128)S(1)} %get-tuple-element.6), channel_id=1, replica_groups=mesh['fsdp'=8,'tp'=4] {'tp'}, use_global_device_ids=true, to_apply=%region_1.2 | all-reduce | flops 4096 | bytes 32768 | tf_op jit(solution)/shard_map/psum | solution.py:38
  102.5 0.0 copy-done.4
  102.5 0.0 copy-start.3
  102.5 12.2 %multiply_convert_fusion.1 = bf16[2,2048,1024]{2,1,0:T(8,128)(2,1)} fusion(f32[2,2048,1024]{2,1,0:T(8,128)} %get-tuple-element.5, bf16[2,2048,1024]{2,1,0:T(8,128)(2,1)} %param.8, f32[2,1024]{1,0:T(2,128)S(1)} %get-tuple-element.9, f32[2,1024]{1,0:T(2,128)S(1)} %copy-done.4), kind=kLoop, calls=%fused_computation.3 | loop fusion | flops 25165824 | bytes 33570816 | tf_op jit(solution)/shard_map/convert_element_type | solution.py:17
  114.7 0.0 copy-done.3
  114.7 0.0 copy-start.1
  114.7 38.2 %multiply_convert_fusion = bf16[2,7168,1024]{2,1,0:T(8,128)(2,1)} fusion(f32[2,7168,1024]{2,1,0:T(8,128)} %get-tuple-element.7, bf16[2,7168,1024]{2,1,0:T(8,128)(2,1)} %param.9, f32[2,1024]{1,0:T(2,128)S(1)} %get-tuple-element.8, f32[2,1024]{1,0:T(2,128)S(1)} %copy-done.3), kind=kLoop, calls=%fused_computation | loop fusion | flops 88080384 | bytes 117456896 | tf_op jit(solution)/shard_map/convert_element_type | solution.py:17
  152.8 0.0 copy-done.1
  (2 shorter events, 0.0 us)
Async XLA Ops:
  7.2 1.2 copy-start
  7.2 54.3 %copy-start.2 = (bf16[2,1024,64]{1,2,0:T(8,128)(2,1)S(1)}, bf16[2,1024,64]{1,2,0:T(8,128)(2,1)}, u32[]{:S(2)}) copy-start(bf16[2,1024,64]{1,2,0:T(8,128)(2,1)} %param.13) | copy-start | bytes 786436
  7.2 54.3 %all-gather.4.cloned.1.call-start = ((), (), s32[]{:S(2)}) async-start(), calls=%async_computation | async-start | bytes 2064384 | tf_op jit(solution)/shard_map/all_gather | solution.py:36
  54.5 48.0 %copy-start.4 = (f32[2,1024]{1,0:T(2,128)S(1)}, f32[2,1024]{1,0:T(2,128)}, u32[]{:S(2)}) copy-start(f32[2,1024]{1,0:T(2,128)} %param.14) | copy-start | bytes 24580
  102.5 12.2 %copy-start.3 = (f32[2,1024]{1,0:T(2,128)S(1)}, f32[2,1024]{1,0:T(2,128)}, u32[]{:S(2)}) copy-start(f32[2,1024]{1,0:T(2,128)} %param.15) | copy-start | bytes 24580
  114.7 38.2 %copy-start.1 = (bf16[2,64,4,896]{3,2,1,0:T(4,128)(2,1)S(1)}, bf16[2,64,4,896]{3,2,1,0:T(4,128)(2,1)}, u32[]{:S(2)}) copy-start(bf16[2,64,4,896]{3,2,1,0:T(4,128)(2,1)} %param.12) | copy-start | bytes 2752516
Sparse Core Ops, SparseCore 0:
  10.8 50.6 all-gather.3
where the time goes:
time: 160 us
  other arithmetic  50.4 us (32%)
  blocking collectives  43.8 us (27%)
  matrix products  40.9 us (26%)
  between operations  14.1 us (9%)
  waiting for transfers between devices  7.03 us (4%)
  local copies, waits for them, and re-layouts  3.44 us (2%)
    convert_element_type x2, other arithmetic, finish(): (magnitude[:, None, :] * summed * lax.rsqrt(square + 1e-06)[:, None, :])....  50.4 us
    dot_general x2, matrix products, low_rank(): jnp.einsum('lri,lor->lio', rows_a, factor_b, preferred_element_type=jnp.f...  40.9 us
    all_gather x1, blocking collectives, local(): lax.all_gather(own_o, 'fsdp', axis=2, tiled=True)  33.7 us
    psum x1, blocking collectives, local(): square_o = lax.psum(partial_o, 'tp')  10.1 us
    all_gather x1, waiting for transfers between devices, local(): lax.all_gather(own_down, 'fsdp', axis=2, tiled=True)  7.01 us
  transfers between devices with their start and end apart: 1, of which 1 were waited for; matrix products, arithmetic and copies ran while one was open for 7% of the time, Pallas kernels for 0%

commit v1 on v0

v1 whole, which is shorter than its diff:
```python
import functools

import jax
import jax.numpy as jnp
from jax import lax
from jax.experimental import pallas as pl
from jax.experimental.pallas import tpu as pltpu
from jax.sharding import PartitionSpec as P

MESH = pl.DeviceIdType.MESH
F32 = jnp.float32
BF16 = jnp.bfloat16


def row_tile(rows, most):
    return max(t for t in range(16, most + 1, 16) if rows % t == 0)


def gather_kernel(
    n,
    n_tp,
    sizes,
    rank,
    base_o,
    base_d,
    a_o,
    a_d,
    b_o,
    b_d,
    mag_o,
    mag_d,
    held_o,
    held_d,
    full_a,
    weights,
    scale,
    block,
    acc,
    sums,
    peers,
    read_sem,
    own_sem,
    send_sem,
    recv_sem,
    sum_send,
    sum_recv,
):
    layers, columns = mag_o.shape
    depth = n // 2
    me, t = lax.axis_index("fsdp"), lax.axis_index("tp")
    z, y = me // 2, me % 2
    other = z * 2 + 1 - y
    has_lo, has_hi = z > 0, z < depth - 1

    def to_fsdp(f):
        return {"fsdp": f}

    barrier = pltpu.get_barrier_semaphore()

    def greet(device):
        pl.semaphore_signal(barrier, inc=1, device_id=device, device_id_type=MESH)

    greet(to_fsdp(other))
    for k in range(1, n_tp):
        greet({"tp": (t + k) % n_tp})
    pl.when(has_lo)(lambda: greet(to_fsdp(me - 2)))
    pl.when(has_hi)(lambda: greet(to_fsdp(me + 2)))

    def slot_of(e, lo, side):
        return (z - e if lo else z + e) * 2 + side

    bases = (base_o, base_d)
    helds = (held_o, held_d)
    starts = (0, sizes[0])

    def read(p, layer, f):
        rows = pl.ds(pl.multiple_of(f * sizes[p], 16), sizes[p])
        return pltpu.make_async_copy(
            bases[p].at[layer, rows], helds[p].at[layer, rows], read_sem.at[p, layer, f]
        )

    def read_slot(f):
        for p in range(2):
            for layer in range(layers):
                read(p, layer, f).start()

    read_slot(me)
    read_slot(other)

    @pl.loop(1, depth)
    def _(d):
        for side in (y, 1 - y):
            pl.when(z - d >= 0)(lambda: read_slot(slot_of(d, True, side)))
            pl.when(z + d < depth)(lambda: read_slot(slot_of(d, False, side)))

    for p, a in enumerate((a_o, a_d)):
        parts = []
        for layer in range(layers):
            rows = a[layer, :, 0, :].astype(F32)
            for u in range(1, n_tp):
                rows = jnp.where(t == u, a[layer, :, u, :].astype(F32), rows)
            parts.append(rows)
        block[pl.ds(starts[p], sizes[p]), :] = jnp.concatenate(parts, axis=0).T.astype(BF16)

    ends = has_lo.astype(jnp.int32) + has_hi.astype(jnp.int32)
    pl.semaphore_wait(barrier, n_tp + ends)

    def send(source, f, way, target):
        return pltpu.make_async_remote_copy(
            src_ref=source,
            dst_ref=full_a.at[f],
            send_sem=send_sem.at[way, f],
            recv_sem=recv_sem.at[f],
            device_id=to_fsdp(target),
            device_id_type=MESH,
        )

    def arrived(f):
        send(full_a.at[f], f, 0, other).wait_recv()

    pl.when(has_lo)(lambda: send(block, me, 1, me - 2).start())
    pl.when(has_hi)(lambda: send(block, me, 2, me + 2).start())
    send(block, me, 0, other).start()
    own = pltpu.make_async_copy(block, full_a.at[me], own_sem)
    own.start()

    for p, b in enumerate((b_o, b_d)):
        for layer in range(layers):
            weights[p, layer] = jnp.zeros((layers * rank, columns), BF16)
            weights[p, layer, pl.ds(layer * rank, rank), :] = (
                b[layer].astype(F32) * 0.25
            ).astype(BF16)
    acc[...] = jnp.zeros_like(acc)
    own.wait()

    wide = 256 if columns % 256 == 0 else columns

    def process(f):
        for p in range(2):
            tile = row_tile(sizes[p], 256)

            @pl.loop(0, layers)
            def _(layer):
                read(p, layer, f).wait()

                @pl.loop(0, sizes[p] // tile)
                def _(i):
                    rows = pl.ds(pl.multiple_of(starts[p] + i * tile, 16), tile)
                    held = pl.ds(pl.multiple_of(f * sizes[p] + i * tile, 16), tile)
                    left = full_a[f, rows, :]
                    for c in range(0, columns, wide):
                        cut = pl.ds(c, wide)
                        total = jnp.dot(
                            left, weights[p, layer, :, cut], preferred_element_type=F32
                        ) + helds[p][layer, held, cut].astype(F32)
                        acc[p, layer, :, cut] += jnp.sum(
                            (total * total).reshape(tile // 8, 8, wide), axis=0
                        )

    def from_other(e):
        def take(f):
            arrived(f)
            process(f)

        pl.when(z - e >= 0)(lambda: take(slot_of(e, True, 1 - y)))
        pl.when((e > 0) & (z + e < depth))(lambda: take(slot_of(e, False, 1 - y)))

    process(me)

    @pl.loop(1, depth)
    def _(d):
        @pl.when(z - d >= 0)
        def _():
            f = slot_of(d, True, y)
            arrived(f)
            pl.when(has_hi)(lambda: send(full_a.at[f], f, 2, me + 2).start())
            send(full_a.at[f], f, 0, other).start()

        @pl.when(z + d < depth)
        def _():
            f = slot_of(d, False, y)
            arrived(f)
            pl.when(has_lo)(lambda: send(full_a.at[f], f, 1, me - 2).start())
            send(full_a.at[f], f, 0, other).start()

        from_other(d - 1)
        pl.when(z - d >= 0)(lambda: process(slot_of(d, True, y)))
        pl.when(z + d < depth)(lambda: process(slot_of(d, False, y)))

    from_other(jnp.int32(depth - 1))

    for p in range(2):
        for layer in range(layers):
            sums[p * layers + layer, :] = jnp.sum(acc[p, layer], axis=0)

    pl.when(has_lo)(lambda: send(block, me, 1, me - 2).wait_send())
    pl.when(has_hi)(lambda: send(block, me, 2, me + 2).wait_send())
    send(block, me, 0, other).wait_send()

    @pl.loop(1, depth)
    def _(d):
        @pl.when(z - d >= 0)
        def _():
            f = slot_of(d, True, y)
            pl.when(has_hi)(lambda: send(full_a.at[f], f, 2, me + 2).wait_send())
            send(full_a.at[f], f, 0, other).wait_send()

        @pl.when(z + d < depth)
        def _():
            f = slot_of(d, False, y)
            pl.when(has_lo)(lambda: send(full_a.at[f], f, 1, me - 2).wait_send())
            send(full_a.at[f], f, 0, other).wait_send()

    def share(k):
        return pltpu.make_async_remote_copy(
            src_ref=sums,
            dst_ref=peers.at[k - 1],
            send_sem=sum_send.at[k - 1],
            recv_sem=sum_recv.at[k - 1],
            device_id={"tp": (t + k) % n_tp},
            device_id_type=MESH,
        )

    for k in range(1, n_tp):
        share(k).start()
    square = sums[...]
    for k in range(1, n_tp):
        share(k).wait()
    for k in range(1, n_tp):
        square = square + peers[k - 1]
    magnitude = jnp.concatenate([mag_o[...], mag_d[...]], axis=0)
    scale[...] = magnitude * lax.rsqrt(square + 1e-06)


def finish_kernel(sizes, held_o, held_d, full_a, weights, scale, out_o, out_d):
    layers, _, columns = held_o.shape
    layer, f = pl.program_id(0), pl.program_id(1)
    wide = 256 if columns % 256 == 0 else columns
    for p, (held, out) in enumerate(((held_o, out_o), (held_d, out_d))):
        size, start = sizes[p], sum(sizes[:p])
        tile = row_tile(size, 256)
        factor = scale[pl.ds(p * layers + layer, 1), :]

        @pl.loop(0, size // tile)
        def _(i):
            rows = pl.ds(pl.multiple_of(start + i * tile, 16), tile)
            inside = pl.ds(pl.multiple_of(f * size + i * tile, 16), tile)
            here = pl.ds(pl.multiple_of(i * tile, 16), tile)
            left = full_a[f, rows, :]
            for c in range(0, columns, wide):
                cut = pl.ds(c, wide)
                total = jnp.dot(
                    left, weights[p, layer, :, cut], preferred_element_type=F32
                ) + held[layer, inside, cut].astype(F32)
                out[0, here, cut] = (total * factor[:, c : c + wide]).astype(BF16)


def solution(mesh):
    n, n_tp = mesh.shape["fsdp"], mesh.shape["tp"]
    in_vmem = pl.BlockSpec(memory_space=pltpu.VMEM)
    anywhere = pl.BlockSpec(memory_space=pl.ANY)

    def local(base_o, base_d, a_o, b_o, a_d, b_d, mag_o, mag_d):
        layers, rank, _, part_o = a_o.shape
        sizes = (part_o, a_d.shape[3])
        columns = base_o.shape[2]
        depth = layers * rank
        base_o = pltpu.with_memory_space_constraint(base_o, pltpu.HBM)
        base_d = pltpu.with_memory_space_constraint(base_d, pltpu.HBM)
        shapes = (
            pltpu.VMEM(base_o.shape, BF16),
            pltpu.VMEM(base_d.shape, BF16),
            pltpu.VMEM((n, sum(sizes), depth), BF16),
            pltpu.VMEM((2, layers, depth, columns), BF16),
            pltpu.VMEM((2 * layers, columns), F32),
        )
        held_o, held_d, full_a, weights, scale = pl.pallas_call(
            functools.partial(gather_kernel, n, n_tp, sizes, rank),
            out_shape=shapes,
            in_specs=[anywhere] * 2 + [in_vmem] * 6,
            out_specs=[in_vmem] * 5,
            scratch_shapes=[
                pltpu.VMEM((sum(sizes), depth), BF16),
                pltpu.VMEM((2, layers, 8, columns), F32),
                pltpu.VMEM((2 * layers, columns), F32),
                pltpu.VMEM((n_tp - 1, 2 * layers, columns), F32),
                pltpu.SemaphoreType.DMA((2, layers, n)),
                pltpu.SemaphoreType.DMA,
                pltpu.SemaphoreType.DMA((3, n)),
                pltpu.SemaphoreType.DMA((n,)),
                pltpu.SemaphoreType.DMA((n_tp - 1,)),
                pltpu.SemaphoreType.DMA((n_tp - 1,)),
            ],
            compiler_params=pltpu.CompilerParams(
                collective_id=0, has_side_effects=True, vmem_limit_bytes=20 << 20
            ),
            name="gather_squares",
        )(
            base_o, base_d, a_o, a_d, b_o.swapaxes(1, 2), b_d.swapaxes(1, 2), mag_o, mag_d
        )

        kept = [
            pltpu.with_memory_space_constraint(x, pltpu.VMEM)
            for x in (held_o, held_d, full_a, weights, scale)
        ]
        return pl.pallas_call(
            functools.partial(finish_kernel, sizes),
            out_shape=[jax.ShapeDtypeStruct(b.shape, BF16) for b in (base_o, base_d)],
            grid=(layers, n),
            in_specs=[in_vmem] * 5,
            out_specs=[
                pl.BlockSpec((1, size, columns), lambda i, f: (i, f, 0)) for size in sizes
            ],
            compiler_params=pltpu.CompilerParams(vmem_limit_bytes=20 << 20),
            name="finish",
        )(*kept)

    return jax.shard_map(
        local,
        mesh=mesh,
        in_specs=(
            P(None, "tp", "fsdp"),
            P(None, "tp", "fsdp"),
            P(None, None, None, "fsdp"),
            P(None, "fsdp", None),
            P(None, None, None, "fsdp"),
            P(None, "fsdp", None),
            P(None, "fsdp"),
            P(None, "fsdp"),
        ),
        out_specs=(P(None, "tp", "fsdp"), P(None, "tp", "fsdp")),
        check_vma=False,
    )
```

time: 160 us -> 66.8 us (0.42)
  Pallas kernels: 0 us -> 66 us
  other arithmetic: 50.4 us -> 0 us
  blocking collectives: 43.8 us -> 0 us
  matrix products: 40.9 us -> 0 us
  between operations: 14.1 us -> 0.64 us
  waiting for transfers between devices: 7.03 us -> 0 us
  local copies, waits for them, and re-layouts: 3.44 us -> 0 us
    pallas_call x0 -> x2, Pallas kernels: none -> 66 us  [the longest x1 42.5 us: local(): pl.pallas_call(functools.partial(gather_kernel, n, n_tp, sizes, rank), ou...]
    convert_element_type x2 -> x0, other arithmetic: 50.4 us -> none  [finish(): (magnitude[:, None, :] * summed * lax.rsqrt(square + 1e-06)[:, None, :])....]
    dot_general x2 -> x0, matrix products: 40.9 us -> none  [low_rank(): jnp.einsum('lri,lor->lio', rows_a, factor_b, preferred_element_type=jnp.f...]
    all_gather x1 -> x0, blocking collectives: 33.7 us -> none  [local(): lax.all_gather(own_o, 'fsdp', axis=2, tiled=True)]
    psum x1 -> x0, blocking collectives: 10.1 us -> none  [local(): square_o = lax.psum(partial_o, 'tp')]
    all_gather x1 -> x0, waiting for transfers between devices: 7.01 us -> none  [local(): lax.all_gather(own_down, 'fsdp', axis=2, tiled=True)]
    unnamed x12 -> x0, local copies, waits for them, and re-layouts: 1.86 us -> none
  transfers between devices with their start and end apart: 1 -> 0, of which waited for: 1 -> 0; matrix products, arithmetic and copies ran while one was open for 7% -> 0% of each run, Pallas kernels for 0% -> 0%
where the time goes in v1:
time: 66.8 us; the launch traced here: 66.7 us
  Pallas kernels  66 us (99%)
    pallas_call x1, Pallas kernels, local(): pl.pallas_call(functools.partial(gather_kernel, n, n_tp, sizes, rank), ou...  42.5 us
    pallas_call x1, Pallas kernels, local(): pl.pallas_call(functools.partial(finish_kernel, sizes), out_shape=[jax.Sh...  23.5 us

profile of v1, /device:TPU:0, one launch (start us, length us, event | category | flops | bytes accessed | tf_op | source)
XLA Modules:
  0.0 66.7 jit_solution(10906402798715115822)
XLA Ops:
  0.6 42.5 %gather_squares.1 = (bf16[2,2048,1024]{2,1,0:T(8,128)(2,1)S(1)}, bf16[2,7168,1024]{2,1,0:T(8,128)(2,1)S(1)}, bf16[8,1152,128]{2,1,0:T(8,128)(2,1)S(1)}, bf16[2,2...) custom-call(bf16[2,2048,1024]{2,1,0:T(8,128)(2,1)} %base_o.1, bf16[2,7168,1024]{2,1,0:T(8,128)(2,1)} %base_d.1, ...), custom_call_target="tpu_custom_call" | custom-call | tf_op jit(solution)/shard_map/gather_squares/pallas_call | solution.py:277
  43.2 23.5 %finish.1 = (bf16[2,2048,1024]{2,1,0:T(8,128)(2,1)}, bf16[2,7168,1024]{2,1,0:T(8,128)(2,1)}) custom-call(bf16[2,2048,1024]{2,1,0:T(8,128)(2,1)S(1)} %get-tuple-element.7.held_o, bf16[2,7168,1024]{2,1,0:T(8,128)(2,1)S(1)} %get-tuple-element.8.held_d, bf16[8,1152,128]{2,1,0:T(8,128)(2,1)S(1)} %get-tuple-element.9.full_a, ...), custom_call_target="tpu_custom_call" | custom-call | tf_op jit(solution)/shard_map/finish/pallas_call | solution.py:306
